TPU v7x, 32 devices: a whole 2x2x4 slice. The times are simulated.
32 devices in a mesh: row: 4 (over z), col: 2 (over y), depth: 4 (over x, core).
Axes of the slice: x: 2, y: 2, z: 4, core: 2. Of those that a mesh axis runs over, the one named last changes fastest.
Arguments:
- a21_leaf: float32 [4, 4096, 2048], P('depth', 'row', 'col'), may hold values from -1.2 to 1.2
- a12_leaf: float32 [4, 2048, 4096], P('depth', 'row', 'col'), may hold values from -1.2 to 1.2
- uinv_leaf: float32 [4, 2048, 2048], P('depth', None, 'col'), may hold values from -0.2 to 1.5, as said below
- linv_leaf: float32 [4, 2048, 2048], P('depth', 'row'), may hold values from -0.2 to 1.5, as said below
- live: int32 [4], P('depth'), may hold values from 16 to 32
- row_map: int32 [4, 32], P('depth', 'row'), may hold values from 0 to 63, as said below
- col_map: int32 [4, 32], P('depth', 'col'), may hold values from 0 to 63, as said below
- a22_anc: float32 [8192, 8192], P(('row', 'depth'), 'col'), may hold values from -6 to 6
- a21_anc: float32 [8192, 2048], P(('row', 'depth'), 'col'), may hold values from -1.2 to 1.2
- a12_anc: float32 [2048, 8192], P(('row', 'depth'), 'col'), may hold values from -1.2 to 1.2
- uinv_anc: float32 [2048, 2048], P(None, 'col'), may hold values from -0.2 to 1.5, as said below
- linv_anc: float32 [2048, 2048], P(('row', 'depth')), may hold values from -0.2 to 1.5, as said below
Outputs:
- leaf_lower: float32 [4, 4096, 2048], P('depth', 'row', 'col')
- leaf_upper: float32 [4, 2048, 4096], P('depth', 'row', 'col')
- anc_lower: float32 [8192, 2048], P(('row', 'depth'), 'col')
- anc_upper: float32 [2048, 8192], P(('row', 'depth'), 'col')
- anc_schur: float32 [8192, 8192], P(('row', 'depth'), 'col')
Inputs may be any that keep to these rules, and one draw needn't show every extreme that they name: `uinv_leaf`: upper triangular: zero below the diagonal, diagonal between 0.5 and 1.5. `linv_leaf`: lower triangular: zero above the diagonal, diagonal between 0.5 and 1.5. `uinv_anc`: upper triangular: zero below the diagonal, diagonal between 0.5 and 1.5. `linv_anc`: lower triangular: zero above the diagonal, diagonal between 0.5 and 1.5. `row_map`: within one replica the entries are distinct. Leaf block row i lies in the k-th of 4 equal ranges of leaf block rows, and its target lies in the k-th of 4 equal ranges of the 64 ancestor block rows. `col_map`: within one replica the entries are distinct. Leaf block column j lies in the k-th of 2 equal ranges of leaf block columns, and its target lies in the k-th of 2 equal ranges of the 64 ancestor block columns.
All inputs are finite; a program needn't handle non-finite values.
Results may differ from a plain program's by a relative error of at most 0.0001.
Values sent between devices are 32-bit elements; how exact they have to be, the bound alone decides.
A program may use at most 256 MiB of HBM per device.

v0:
```python
import jax
import jax.numpy as jnp
from jax import lax
from jax.sharding import PartitionSpec as P

NB = 128


def product(left, right):
    return jnp.dot(left, right, precision=lax.Precision.HIGHEST, preferred_element_type=jnp.float32)


def reduce_depth(update):
    return lax.psum_scatter(update, "depth", scatter_dimension=0, tiled=True)


def combine_depth(schur, row_map, col_map, a22_anc):
    block_size = NB
    rows_here = schur.shape[0]
    cols_here = schur.shape[1]
    leaf_rows = rows_here // block_size
    leaf_cols = cols_here // block_size
    anc_rows = a22_anc.shape[0]
    replicas = lax.axis_size("depth")
    anc_row_blocks = anc_rows * replicas // block_size
    anc_col_blocks = a22_anc.shape[1] // block_size
    row_local = row_map[0] - lax.axis_index("row") * anc_row_blocks
    col_local = col_map[0] - lax.axis_index("col") * anc_col_blocks
    col_pick = (col_local[:, None] == lax.iota(jnp.int32, anc_col_blocks)[None, :]).astype(
        jnp.float32
    )
    row_pick = (row_local[:, None] == lax.iota(jnp.int32, anc_row_blocks)[None, :]).astype(
        jnp.float32
    )
    leaf_blocks = schur.reshape(leaf_rows, block_size, leaf_cols, block_size)
    placed = jnp.einsum("ia,ixjy->axjy", row_pick, leaf_blocks, precision=lax.Precision.HIGHEST)
    placed = jnp.einsum("axjy,jb->axby", placed, col_pick, precision=lax.Precision.HIGHEST)
    update = placed.reshape(anc_row_blocks * block_size, anc_col_blocks * block_size)
    return reduce_depth(update)


def anc_panels(a21_anc, a12_anc, uinv_anc, linv_anc):
    factor = uinv_anc
    anc_lower = product(lax.all_gather(a21_anc, "col", axis=1, tiled=True), factor)
    lower_whole = lax.all_gather(anc_lower, "col", axis=1, tiled=True)
    factor = linv_anc
    anc_upper = product(factor, lax.all_gather(a12_anc, ("row", "depth"), axis=0, tiled=True))
    return (anc_lower, lower_whole, anc_upper)


def shards(
    a21_leaf,
    a12_leaf,
    uinv_leaf,
    linv_leaf,
    live,
    row_map,
    col_map,
    a22_anc,
    a21_anc,
    a12_anc,
    uinv_anc,
    linv_anc,
):
    block_size = NB
    panel_left = a21_leaf[0]
    panel_top = a12_leaf[0]
    upper_inverse = uinv_leaf[0]
    lower_inverse = linv_leaf[0]
    rows_here = panel_left.shape[0]
    cols_here = panel_top.shape[1]
    live_rows = live[0] * block_size
    row_pos = lax.axis_index("row") * rows_here + lax.iota(jnp.int32, rows_here)
    col_pos = lax.axis_index("col") * cols_here + lax.iota(jnp.int32, cols_here)
    row_keep = (row_pos < live_rows).astype(jnp.float32)
    col_keep = (col_pos < live_rows).astype(jnp.float32)
    factor = upper_inverse
    lower_part = product(lax.all_gather(panel_left, "col", axis=1, tiled=True), factor)
    leaf_lower = lower_part * row_keep[:, None]
    factor = lower_inverse
    upper_part = product(factor, lax.all_gather(panel_top, "row", axis=0, tiled=True))
    leaf_upper = upper_part * col_keep[None, :]
    upper_whole = lax.all_gather(leaf_upper, "row", axis=0, tiled=True)
    factor = upper_whole
    schur = jnp.zeros((rows_here, cols_here), jnp.float32) - product(
        lax.all_gather(leaf_lower, "col", axis=1, tiled=True), factor
    )
    own_update = combine_depth(schur, row_map, col_map, a22_anc)
    anc_lower, lower_whole, anc_upper = anc_panels(a21_anc, a12_anc, uinv_anc, linv_anc)
    factor = lower_whole
    anc_schur = (
        a22_anc
        + own_update
        - product(factor, lax.all_gather(anc_upper, ("row", "depth"), axis=0, tiled=True))
    )
    return (leaf_lower[None], leaf_upper[None], anc_lower, anc_upper, anc_schur)


def solution(mesh):
    in_specs = (
        P("depth", "row", "col"),
        P("depth", "row", "col"),
        P("depth", None, "col"),
        P("depth", "row", None),
        P("depth"),
        P("depth", "row"),
        P("depth", "col"),
        P(("row", "depth"), "col"),
        P(("row", "depth"), "col"),
        P(("row", "depth"), "col"),
        P(None, "col"),
        P(("row", "depth"), None),
    )
    out_specs = (
        P("depth", "row", "col"),
        P("depth", "row", "col"),
        P(("row", "depth"), "col"),
        P(("row", "depth"), "col"),
        P(("row", "depth"), "col"),
    )
    return jax.shard_map(shards, mesh=mesh, in_specs=in_specs, out_specs=out_specs, check_vma=False)
```

profile of v0, /device:TPU:0, one launch (start us, length us, event | category | flops | bytes accessed | tf_op | source)
XLA Modules:
  0.0 1554.8 jit_solution(6377144033500188488)
XLA Ops:
  7.2 0.0 copy-start
  7.2 0.0 all-gather.23.cloned.1.call-start
  7.2 0.7 all-gather.23.cloned.1.call-update
  7.9 0.0 all-gather.25.cloned.1.call-start
  8.0 0.7 all-gather.25.cloned.1.call-update
  8.7 0.0 all-gather.11.cloned.1.call-start
  8.7 0.7 all-gather.11.cloned.1.call-update
  9.4 0.0 all-gather.15.cloned.1.call-start
  10.1 106.2 %all-gather.23.cloned.1.call-done = f32[1,1024,2048]{2,1,0:T(8,128)} async-done(((f32[1,1024,1024]{2,1,0:T(8,128)}), f32[1,1024,2048]{2,1,0:T(8,128)}) %all-gather.23.cloned.1.call-update) | async-done | bytes 8388624 | tf_op jit(solution)/shard_map/all_gather | solution.py:78
  116.3 31.9 %fusion.15 = f32[1024,1024]{1,0:T(8,128)} fusion(f32[1,2048,1024]{2,1,0:T(8,128)} %param.14, f32[1,1024,2048]{2,1,0:T(8,128)} %all-gather.23.cloned.1.call-done, f32[1024]{0:T(1024)S(1)} %fusion.24), kind=kOutput, calls=%fused_computation.14 | convolution fusion | flops 25770852352 | bytes 20975616 | tf_op jit(solution)/shard_map/dot_general | solution.py:10
  148.1 0.0 all-gather.15.cloned.1.call-update
  148.2 0.0 all-gather.17.cloned.1.call-start
  148.2 0.0 copy-start.1
  148.2 0.0 copy-start.2
  148.3 256.4 %all-gather.25.cloned.1.call-done = f32[1,2048,2048]{2,1,0:T(8,128)} async-done(((f32[1,512,2048]{2,1,0:T(8,128)}), f32[1,2048,2048]{2,1,0:T(8,128)}) %all-gather.25.cloned.1.call-update) | async-done | bytes 16777232 | tf_op jit(solution)/shard_map/all_gather | solution.py:81
  404.6 32.8 %fusion.10 = f32[512,2048]{1,0:T(8,128)} fusion(f32[1,2048,2048]{2,1,0:T(8,128)} %all-gather.25.cloned.1.call-done, f32[1,512,2048]{2,1,0:T(8,128)} %param.15, f32[2048]{0:T(1024)S(1)} %fusion.20), kind=kOutput, calls=%fused_computation.13 | convolution fusion | flops 25770852352 | bytes 25174016 | tf_op jit(solution)/shard_map/dot_general | solution.py:10
  437.5 0.0 all-gather.17.cloned.1.call-update
  437.5 0.0 all-gather.13.cloned.1.call-start
  437.5 0.5 all-gather.13.cloned.1.call-update
  438.1 0.3 all-gather.19.cloned.1.call-start
  438.4 0.0 copy-done.1
  438.4 0.0 copy-done.2
  438.4 22.7 %all-gather.11.cloned.1.call-done = f32[512,2048]{1,0:T(8,128)} async-done(((f32[512,1024]{1,0:T(8,128)}), f32[512,2048]{1,0:T(8,128)}) %all-gather.11.cloned.1.call-update) | async-done | bytes 4194320 | tf_op jit(solution)/shard_map/all_gather | solution.py:44
  461.1 17.5 %fusion.28 = f32[512,1024]{1,0:T(8,128)} fusion(f32[512,2048]{1,0:T(8,128)} %all-gather.11.cloned.1.call-done, f32[2048,1024]{1,0:T(8,128)} %param.22), kind=kOutput, calls=%fused_computation.27 | convolution fusion | flops 12884901888 | bytes 14680064 | tf_op jit(solution)/shard_map/dot_general | solution.py:10
  478.7 0.0 all-gather.19.cloned.1.call-update
  478.7 0.0 reduce-scatter.2.cloned.1.call-start
  478.7 88.4 %all-gather.15.cloned.1.call-done = f32[1024,2048]{1,0:T(8,128)} async-done(((f32[1024,1024]{1,0:T(8,128)}), f32[1024,2048]{1,0:T(8,128)}) %all-gather.15.cloned.1.call-update) | async-done | bytes 8388624 | tf_op jit(solution)/shard_map/all_gather | solution.py:86
  567.1 288.8 %all-gather.17.cloned.1.call-done = f32[2048,2048]{1,0:T(8,128)} async-done(((f32[512,2048]{1,0:T(8,128)}), f32[2048,2048]{1,0:T(8,128)}) %all-gather.17.cloned.1.call-update) | async-done | bytes 16777232 | tf_op jit(solution)/shard_map/all_gather | solution.py:83
  855.9 69.7 %subtract_bitcast_fusion = f32[128,8,16,128]{3,1,2,0:T(8,128)S(1)} fusion(f32[1024,2048]{1,0:T(8,128)} %all-gather.15.cloned.1.call-done, f32[2048,2048]{1,0:T(8,128)} %all-gather.17.cloned.1.call-done), kind=kOutput, calls=%fused_computation.11 | convolution fusion | flops 51541704704 | bytes 33554432 | tf_op jit(solution)/shard_map/dot_general | solution.py:10
  925.6 2.0 copy.21
  927.6 9.7 fusion.7
  937.4 21.8 %fusion.2 = f32[32,16,128,128]{3,0,2,1:T(8,128)} fusion(f32[16,128,16,128]{3,0,2,1:T(8,128)S(1)} %fusion.7, s32[16]{0:T(128)S(1)} %subtract_bitcast_fusion.2), kind=kOutput, calls=%fused_computation.3 | convolution fusion | flops 1610613248 | bytes 50331712 | tf_op jit(solution)/shard_map/axjy,jb->axby/dot_general | solution.py:37
  959.2 38.4 %copy.28 = f32[256,8,32,128]{3,1,2,0:T(8,128)} copy(f32[256,8,32,128]{3,2,1,0:T(8,128)} %bitcast.56) | data formatting | bytes 67108864
  997.5 0.0 reduce-scatter.2.cloned.1.call-update
  997.5 0.0 all-gather.21.cloned.1.call-start
  997.6 26.0 %all-gather.13.cloned.1.call-done = f32[2048,4096]{1,0:T(8,128)} async-done(((f32[128,4096]{1,0:T(8,128)}), f32[2048,4096]{1,0:T(8,128)}) %all-gather.13.cloned.1.call-update) | async-done | bytes 33554448 | tf_op jit(solution)/shard_map/all_gather | solution.py:47
  1023.6 0.0 copy-done
  1023.6 22.6 %fusion.29 = f32[128,4096]{1,0:T(8,128)} fusion(f32[128,2048]{1,0:T(8,128)S(1)} %copy-done, f32[2048,4096]{1,0:T(8,128)} %all-gather.13.cloned.1.call-done), kind=kOutput, calls=%fused_computation.28 | convolution fusion | flops 12884901888 | bytes 36700160 | tf_op jit(solution)/shard_map/dot_general | solution.py:10
  1046.1 0.0 all-gather.21.cloned.1.call-update
  1046.2 36.3 %all-gather.19.cloned.1.call-done = f32[512,2048]{1,0:T(8,128)} async-done(((f32[512,1024]{1,0:T(8,128)}), f32[512,2048]{1,0:T(8,128)}) %all-gather.19.cloned.1.call-update) | async-done | bytes 4194320 | tf_op jit(solution)/shard_map/all_gather | solution.py:45
  1082.4 234.9 %reduce-scatter.2.cloned.1.call-done = f32[512,4096]{1,0:T(8,128)} async-done(((f32[2048,4096]{1,0:T(8,128)}), f32[512,4096]{1,0:T(8,128)}) %reduce-scatter.2.cloned.1.call-update) | async-done | bytes 8388624 | tf_op jit(solution)/shard_map/reduce_scatter | solution.py:14
  1317.4 170.3 %all-gather.21.cloned.1.call-done = f32[2048,4096]{1,0:T(8,128)} async-done(((f32[128,4096]{1,0:T(8,128)}), f32[2048,4096]{1,0:T(8,128)}) %all-gather.21.cloned.1.call-update) | async-done | bytes 33554448 | tf_op jit(solution)/shard_map/all_gather | solution.py:94
  1487.6 60.3 %add_subtract_fusion = f32[512,4096]{1,0:T(8,128)} fusion(f32[512,4096]{1,0:T(8,128)} %param.19, f32[512,4096]{1,0:T(8,128)} %reduce-scatter.2.cloned.1.call-done, f32[512,2048]{1,0:T(8,128)} %all-gather.19.cloned.1.call-done, f32[2048,4096]{1,0:T(8,128)} %all-gather.21.cloned.1.call-done), kind=kOutput, calls=%fused_computation.10 | convolution fusion | flops 51543801856 | bytes 62914560 | tf_op jit(solution)/shard_map/dot_general | solution.py:10
  (4 shorter events, 0.0 us)
Async XLA Ops:
  7.2 1016.4 %copy-start = (f32[128,2048]{1,0:T(8,128)S(1)}, f32[128,2048]{1,0:T(8,128)}, u32[]{:S(2)}) copy-start(f32[128,2048]{1,0:T(8,128)} %param.23) | copy-start | bytes 3145732
  7.2 109.1 %all-gather.23.cloned.1.call-start = ((), (), s32[]{:S(2)}) async-start(), calls=%async_computation.8 | async-start | bytes 12582912 | tf_op jit(solution)/shard_map/all_gather | solution.py:78
  7.9 396.7 %all-gather.25.cloned.1.call-start = ((), (), s32[]{:S(2)}) async-start(), calls=%async_computation.9 | async-start | bytes 20971520 | tf_op jit(solution)/shard_map/all_gather | solution.py:81
  8.7 452.5 %all-gather.11.cloned.1.call-start = ((), (), s32[]{:S(2)}) async-start(), calls=%async_computation.1 | async-start | bytes 6291456 | tf_op jit(solution)/shard_map/all_gather | solution.py:44
  9.4 557.7 %all-gather.15.cloned.1.call-start = ((), (), s32[]{:S(2)}) async-start(), calls=%async_computation.3 | async-start | bytes 12582912 | tf_op jit(solution)/shard_map/all_gather | solution.py:86
  148.2 707.7 %all-gather.17.cloned.1.call-start = ((), (), s32[]{:S(2)}) async-start(), calls=%async_computation.4 | async-start | bytes 20971520 | tf_op jit(solution)/shard_map/all_gather | solution.py:83
  148.2 290.1 %copy-start.1 = (s32[1,8]{1,0:T(1,128)S(1)}, s32[1,8]{1,0:T(1,128)}, u32[]{:S(2)}) copy-start(s32[1,8]{1,0:T(1,128)} %param.17) | copy-start | bytes 100
  148.2 290.1 %copy-start.2 = (s32[1,16]{1,0:T(1,128)S(1)}, s32[1,16]{1,0:T(1,128)}, u32[]{:S(2)}) copy-start(s32[1,16]{1,0:T(1,128)} %param.18) | copy-start | bytes 196
  437.5 586.1 %all-gather.13.cloned.1.call-start = ((), (), s32[]{:S(2)}) async-start(), calls=%async_computation.2 | async-start | bytes 35651584 | tf_op jit(solution)/shard_map/all_gather | solution.py:47
  438.1 644.4 %all-gather.19.cloned.1.call-start = ((), (), s32[]{:S(2)}) async-start(), calls=%async_computation.6 | async-start | bytes 6291456 | tf_op jit(solution)/shard_map/all_gather | solution.py:45
  478.7 838.7 %reduce-scatter.2.cloned.1.call-start = ((), (), s32[]{:S(2)}) async-start(), calls=%async_computation.5 | async-start | bytes 41943040 | tf_op jit(solution)/shard_map/reduce_scatter | solution.py:14
  997.5 490.1 %all-gather.21.cloned.1.call-start = ((), (), s32[]{:S(2)}) async-start(), calls=%async_computation.7 | async-start | bytes 35651584 | tf_op jit(solution)/shard_map/all_gather | solution.py:94
Sparse Core Ops, SparseCore 0:
  9.5 106.6 all-gather.22
  117.8 286.7 all-gather.24
  406.2 54.8 all-gather.10
  463.1 103.9 all-gather.14
  569.1 286.7 all-gather.16
  857.3 166.2 all-gather.12
  1025.7 56.6 all-gather.18
  1085.0 232.3 reduce-scatter.1
  1319.6 168.0 all-gather.20
where the time goes:
time: 1560 us; the launch traced here: 1550 us
  waiting for transfers between devices  1230 us (79%)
  matrix products  266 us (17%)
  local copies, waits for them, and re-layouts  40.4 us (3%)
    all_gather x1, waiting for transfers between devices, shards(): upper_whole = lax.all_gather(leaf_upper, 'row', axis=0, tiled=True)  289 us
    all_gather x1, waiting for transfers between devices, shards(): lax.all_gather(panel_top, 'row', axis=0, tiled=True)  256 us
    reduce_scatter x1, waiting for transfers between devices, reduce_depth(): return lax.psum_scatter(update, 'depth', scatter_dimension=0, tiled=True)  235 us
    dot_general x6, matrix products, product(): jnp.dot(left, right, precision=lax.Precision.HIGHEST, preferred_element_t...  235 us
    all_gather x1, waiting for transfers between devices, shards(): lax.all_gather(anc_upper, ('row', 'depth'), axis=0, tiled=True)  170 us
    all_gather x1, waiting for transfers between devices, shards(): lax.all_gather(panel_left, 'col', axis=1, tiled=True)  106 us
    all_gather x1, waiting for transfers between devices, shards(): lax.all_gather(leaf_lower, 'col', axis=1, tiled=True)  88.4 us
    unnamed x8, local copies, waits for them, and re-layouts  40.4 us
  transfers between devices with their start and end apart: 9, of which 9 were waited for; matrix products, arithmetic and copies ran while one was open for 16% of the time, Pallas kernels for 0%

commit v1 on v0

--- a/solution.py
+++ b/solution.py
@@ -80,7 +80,12 @@
     factor = lower_inverse
     upper_part = product(factor, lax.all_gather(panel_top, "row", axis=0, tiled=True))
     leaf_upper = upper_part * col_keep[None, :]
-    upper_whole = lax.all_gather(leaf_upper, "row", axis=0, tiled=True)
+    ring = [leaf_upper]
+    for hop in range(3):
+        ring.append(lax.ppermute(ring[-1], "row", [(dev, (dev + 1) % 4) for dev in range(4)]))
+    upper_whole = jnp.roll(
+        jnp.concatenate(ring[::-1], axis=0), (lax.axis_index("row") + 1) * ring[0].shape[0], axis=0
+    )
     factor = upper_whole
     schur = jnp.zeros((rows_here, cols_here), jnp.float32) - product(
         lax.all_gather(leaf_lower, "col", axis=1, tiled=True), factor

time: 1560 us -> 1500 us (0.962)
  waiting for transfers between devices: 1230 us -> 1150 us
  local copies, waits for them, and re-layouts: 40.4 us -> 72.4 us
    ppermute x0 -> x3, waiting for transfers between devices: none -> 405 us  [shards(): lax.ppermute(ring[-1], 'row', [(dev, (dev + 1) % 4) for dev in range(4)])]
    all_gather x1 -> x0, waiting for transfers between devices: 289 us -> none  [shards(): upper_whole = lax.all_gather(leaf_upper, 'row', axis=0, tiled=True)]
    all_gather x1, waiting for transfers between devices: 88.4 us -> 0.01 us  [shards(): lax.all_gather(leaf_lower, 'col', axis=1, tiled=True)]
    all_gather x1, waiting for transfers between devices: 36.3 us -> 0.02 us  [anc_panels(): lower_whole = lax.all_gather(anc_lower, 'col', axis=1, tiled=True)]
    unnamed x8 -> x23, local copies, waits for them, and re-layouts: 40.4 us -> 70.2 us
    reduce_scatter x1, waiting for transfers between devices: 235 us -> 206 us  [reduce_depth(): return lax.psum_scatter(update, 'depth', scatter_dimension=0, tiled=True)]
    all_gather x1, waiting for transfers between devices: 26 us -> 0.02 us  [anc_panels(): lax.all_gather(a12_anc, ('row', 'depth'), axis=0, tiled=True)]
    all_gather x1, waiting for transfers between devices: 22.7 us -> 0.02 us  [anc_panels(): lax.all_gather(a21_anc, 'col', axis=1, tiled=True)]
  transfers between devices with their start and end apart: 9 -> 11, of which waited for: 9 -> 7; matrix products, arithmetic and copies ran while one was open for 16% -> 18% of each run, Pallas kernels for 0% -> 0%
where the time goes in v1:
time: 1500 us; the launch traced here: 1490 us
  waiting for transfers between devices  1150 us (77%)
  matrix products  259 us (17%)
  local copies, waits for them, and re-layouts  72.4 us (5%)
  between operations  15.2 us (1%)
    ppermute x3, waiting for transfers between devices, shards(): lax.ppermute(ring[-1], 'row', [(dev, (dev + 1) % 4) for dev in range(4)])  405 us
    all_gather x1, waiting for transfers between devices, shards(): lax.all_gather(panel_top, 'row', axis=0, tiled=True)  256 us
    dot_general x6, matrix products, product(): jnp.dot(left, right, precision=lax.Precision.HIGHEST, preferred_element_t...  227 us
    reduce_scatter x1, waiting for transfers between devices, reduce_depth(): return lax.psum_scatter(update, 'depth', scatter_dimension=0, tiled=True)  206 us
    all_gather x1, waiting for transfers between devices, shards(): lax.all_gather(anc_upper, ('row', 'depth'), axis=0, tiled=True)  170 us
    all_gather x1, waiting for transfers between devices, shards(): lax.all_gather(panel_left, 'col', axis=1, tiled=True)  106 us
    unnamed x23, local copies, waits for them, and re-layouts  70.2 us
  transfers between devices with their start and end apart: 11, of which 7 were waited for; matrix products, arithmetic and copies ran while one was open for 18% of the time, Pallas kernels for 0%

profile of v1, /device:TPU:0, one launch (start us, length us, event | category | flops | bytes accessed | tf_op | source)
XLA Modules:
  0.0 1492.4 jit_solution(2068557507456686219)
XLA Ops:
  7.2 0.0 copy-start
  7.2 0.0 all-gather.20.cloned.1.call-start
  7.2 0.7 all-gather.20.cloned.1.call-update
  7.9 0.0 all-gather.22.cloned.1.call-start
  8.0 0.7 all-gather.22.cloned.1.call-update
  8.7 0.0 all-gather.10.cloned.1.call-start
  8.7 0.7 all-gather.10.cloned.1.call-update
  9.4 0.0 all-gather.14.cloned.1.call-start
  10.1 106.2 %all-gather.20.cloned.1.call-done = f32[1,1024,2048]{2,1,0:T(8,128)} async-done(((f32[1,1024,1024]{2,1,0:T(8,128)}), f32[1,1024,2048]{2,1,0:T(8,128)}) %all-gather.20.cloned.1.call-update) | async-done | bytes 8388624 | tf_op jit(solution)/shard_map/all_gather | solution.py:78
  116.3 31.9 %fusion.19 = f32[1024,1024]{1,0:T(8,128)} fusion(f32[1,2048,1024]{2,1,0:T(8,128)} %param.14, f32[1,1024,2048]{2,1,0:T(8,128)} %all-gather.20.cloned.1.call-done, f32[1024]{0:T(1024)S(1)} %fusion.28), kind=kOutput, calls=%fused_computation.16 | convolution fusion | flops 25770852352 | bytes 20975616 | tf_op jit(solution)/shard_map/dot_general | solution.py:10
  148.1 0.0 all-gather.14.cloned.1.call-update
  148.2 0.0 all-gather.12.cloned.1.call-start
  148.2 0.5 all-gather.12.cloned.1.call-update
  148.8 0.2 all-gather.16.cloned.1.call-start
  149.0 0.0 copy-start.5
  149.0 0.0 copy-start.6
  149.0 255.6 %all-gather.22.cloned.1.call-done = f32[1,2048,2048]{2,1,0:T(8,128)} async-done(((f32[1,512,2048]{2,1,0:T(8,128)}), f32[1,2048,2048]{2,1,0:T(8,128)}) %all-gather.22.cloned.1.call-update) | async-done | bytes 16777232 | tf_op jit(solution)/shard_map/all_gather | solution.py:81
  404.6 31.8 %fusion.14 = f32[512,2048]{1,0:T(8,128)S(1)} fusion(f32[1,2048,2048]{2,1,0:T(8,128)} %all-gather.22.cloned.1.call-done, f32[1,512,2048]{2,1,0:T(8,128)} %param.15, f32[2048]{0:T(1024)S(1)} %fusion.24), kind=kOutput, calls=%fused_computation.15 | convolution fusion | flops 25770852352 | bytes 25174016 | tf_op jit(solution)/shard_map/dot_general | solution.py:10
  436.4 0.0 copy-start.1
  436.4 2.0 copy-done.1
  438.4 0.0 collective-permute-start
  438.4 94.3 %collective-permute-done = f32[512,2048]{1,0:T(8,128)S(1)} collective-permute-done((f32[512,2048]{1,0:T(8,128)S(1)}, f32[512,2048]{1,0:T(8,128)S(1)}, u32[]{:S(2)}, u32[]{:S(2)}) %collective-permute-start) | collective-permute-done | bytes 4194336 | tf_op jit(solution)/shard_map/ppermute | solution.py:85
  532.7 0.0 copy-start.3
  532.7 2.0 copy-done.3
  534.7 0.0 collective-permute-start.1
  534.7 144.7 %collective-permute-done.1 = f32[512,2048]{1,0:T(8,128)} collective-permute-done((f32[512,2048]{1,0:T(8,128)S(1)}, f32[512,2048]{1,0:T(8,128)}, u32[]{:S(2)}, u32[]{:S(2)}) %collective-permute-start.1) | collective-permute-done | bytes 4194336 | tf_op jit(solution)/shard_map/ppermute | solution.py:85
  679.4 0.0 collective-permute-start.2
  679.4 0.0 copy-done.5
  679.4 0.0 copy-done.6
  679.5 0.0 all-gather.10.cloned.1.call-done
  679.5 17.6 %fusion.33 = f32[512,1024]{1,0:T(8,128)} fusion(f32[512,2048]{1,0:T(8,128)} %all-gather.10.cloned.1.call-done, f32[2048,1024]{1,0:T(8,128)} %param.22), kind=kOutput, calls=%fused_computation.38 | convolution fusion | flops 12884901888 | bytes 14680064 | tf_op jit(solution)/shard_map/dot_general | solution.py:10
  697.1 0.0 all-gather.16.cloned.1.call-update
  697.1 0.0 reduce-scatter.2.cloned.1.call-start
  697.2 0.0 copy-start.4
  697.2 165.6 %collective-permute-done.2 = f32[512,2048]{1,0:T(8,128)} collective-permute-done((f32[512,2048]{1,0:T(8,128)}, f32[512,2048]{1,0:T(8,128)}, u32[]{:S(2)}, u32[]{:S(2)}) %collective-permute-start.2) | collective-permute-done | bytes 4194336 | tf_op jit(solution)/shard_map/ppermute | solution.py:85
  862.8 4.8 constant_dynamic-update-slice_fusion.7
  867.5 0.0 copy-start.2
  867.5 4.8 constant_dynamic-update-slice_fusion.6
  872.4 0.0 copy-done.4
  872.4 2.2 constant_dynamic-update-slice_fusion.5
  874.6 0.0 copy-done.2
  874.6 2.2 constant_dynamic-update-slice_fusion.4
  876.8 4.7 constant_dynamic-update-slice_fusion.3
  881.6 5.0 constant_dynamic-update-slice_fusion.2
  886.6 2.2 constant_dynamic-update-slice_fusion.1
  888.8 2.2 constant_dynamic-update-slice_fusion
  891.0 0.0 all-gather.14.cloned.1.call-done
  891.0 61.7 %subtract_bitcast_fusion = f32[128,8,16,128]{3,1,2,0:T(8,128)S(1)} fusion(f32[1024,2048]{1,0:T(8,128)} %all-gather.14.cloned.1.call-done, f32[4096,2048]{1,0:T(8,128)} %constant_dynamic-update-slice_fusion, s32[]{:T(128)S(6)} %select_n.14), kind=kOutput, calls=%fused_computation.13 | convolution fusion | flops 51541704704 | bytes 33554436 | tf_op jit(solution)/shard_map/dot_general | solution.py:10
  952.7 2.0 copy.21
  954.7 9.7 fusion.9
  964.4 21.8 %fusion.2 = f32[32,16,128,128]{3,0,2,1:T(8,128)} fusion(f32[16,128,16,128]{3,0,2,1:T(8,128)S(1)} %fusion.9, s32[16]{0:T(128)S(1)} %subtract_bitcast_fusion.2), kind=kOutput, calls=%fused_computation.3 | convolution fusion | flops 1610613248 | bytes 50331712 | tf_op jit(solution)/shard_map/axjy,jb->axby/dot_general | solution.py:37
  986.2 38.1 %copy.28 = f32[256,8,32,128]{3,1,2,0:T(8,128)} copy(f32[256,8,32,128]{3,2,1,0:T(8,128)} %bitcast.57) | data formatting | bytes 67108864
  1024.4 0.0 reduce-scatter.2.cloned.1.call-update
  1024.4 0.0 all-gather.18.cloned.1.call-start
  1024.4 0.0 all-gather.12.cloned.1.call-done
  1024.5 0.0 copy-done
  1024.5 24.2 %fusion.34 = f32[128,4096]{1,0:T(8,128)} fusion(f32[128,2048]{1,0:T(8,128)S(1)} %copy-done, f32[2048,4096]{1,0:T(8,128)} %all-gather.12.cloned.1.call-done), kind=kOutput, calls=%fused_computation.39 | convolution fusion | flops 12884901888 | bytes 36700160 | tf_op jit(solution)/shard_map/dot_general | solution.py:10
  1048.6 0.0 all-gather.18.cloned.1.call-update
  1048.7 0.0 all-gather.16.cloned.1.call-done
  1048.7 206.1 %reduce-scatter.2.cloned.1.call-done = f32[512,4096]{1,0:T(8,128)} async-done(((f32[2048,4096]{1,0:T(8,128)}), f32[512,4096]{1,0:T(8,128)}) %reduce-scatter.2.cloned.1.call-update) | async-done | bytes 8388624 | tf_op jit(solution)/shard_map/reduce_scatter | solution.py:14
  1254.8 170.3 %all-gather.18.cloned.1.call-done = f32[2048,4096]{1,0:T(8,128)} async-done(((f32[128,4096]{1,0:T(8,128)}), f32[2048,4096]{1,0:T(8,128)}) %all-gather.18.cloned.1.call-update) | async-done | bytes 33554448 | tf_op jit(solution)/shard_map/all_gather | solution.py:99
  1425.1 60.3 %add_subtract_fusion = f32[512,4096]{1,0:T(8,128)} fusion(f32[512,4096]{1,0:T(8,128)} %param.19, f32[512,4096]{1,0:T(8,128)} %reduce-scatter.2.cloned.1.call-done, f32[512,2048]{1,0:T(8,128)} %all-gather.16.cloned.1.call-done, f32[2048,4096]{1,0:T(8,128)} %all-gather.18.cloned.1.call-done), kind=kOutput, calls=%fused_computation.12 | convolution fusion | flops 51543801856 | bytes 62914560 | tf_op jit(solution)/shard_map/dot_general | solution.py:10
  (4 shorter events, 0.0 us)
Async XLA Ops:
  7.2 1017.3 %copy-start = (f32[128,2048]{1,0:T(8,128)S(1)}, f32[128,2048]{1,0:T(8,128)}, u32[]{:S(2)}) copy-start(f32[128,2048]{1,0:T(8,128)} %param.23) | copy-start | bytes 3145732
  7.2 109.1 %all-gather.20.cloned.1.call-start = ((), (), s32[]{:S(2)}) async-start(), calls=%async_computation.7 | async-start | bytes 12582912 | tf_op jit(solution)/shard_map/all_gather | solution.py:78
  7.9 396.7 %all-gather.22.cloned.1.call-start = ((), (), s32[]{:S(2)}) async-start(), calls=%async_computation.8 | async-start | bytes 20971520 | tf_op jit(solution)/shard_map/all_gather | solution.py:81
  8.7 670.8 %all-gather.10.cloned.1.call-start = ((), (), s32[]{:S(2)}) async-start(), calls=%async_computation.1 | async-start | bytes 6291456 | tf_op jit(solution)/shard_map/all_gather | solution.py:44
  9.4 881.6 %all-gather.14.cloned.1.call-start = ((), (), s32[]{:S(2)}) async-start(), calls=%async_computation.3 | async-start | bytes 12582912 | tf_op jit(solution)/shard_map/all_gather | solution.py:91
  148.2 876.3 %all-gather.12.cloned.1.call-start = ((), (), s32[]{:S(2)}) async-start(), calls=%async_computation.2 | async-start | bytes 35651584 | tf_op jit(solution)/shard_map/all_gather | solution.py:47
  148.8 899.9 %all-gather.16.cloned.1.call-start = ((), (), s32[]{:S(2)}) async-start(), calls=%async_computation.5 | async-start | bytes 6291456 | tf_op jit(solution)/shard_map/all_gather | solution.py:45
  149.0 530.4 %copy-start.5 = (s32[1,8]{1,0:T(1,128)S(1)}, s32[1,8]{1,0:T(1,128)}, u32[]{:S(2)}) copy-start(s32[1,8]{1,0:T(1,128)} %param.17) | copy-start | bytes 100
  149.0 530.4 %copy-start.6 = (s32[1,16]{1,0:T(1,128)S(1)}, s32[1,16]{1,0:T(1,128)}, u32[]{:S(2)}) copy-start(s32[1,16]{1,0:T(1,128)} %param.18) | copy-start | bytes 196
  436.4 2.0 copy-start.1
  438.4 94.3 %collective-permute-start = (f32[512,2048]{1,0:T(8,128)S(1)}, f32[512,2048]{1,0:T(8,128)S(1)}, u32[]{:S(2)}, u32[]{:S(2)}) collective-permute-start(f32[512,2048]{1,0:T(8,128)S(1)} %fusion.14), channel_id=1, source_target_pairs={{0,8},{8,16},{16,24},{24,0},{1,9},{9,17},{17,25},{25,1},{2,10},{10... | collective-permute-start | bytes 12582920 | tf_op jit(solution)/shard_map/ppermute | solution.py:85
  532.7 2.0 copy-start.3
  534.7 144.7 %collective-permute-start.1 = (f32[512,2048]{1,0:T(8,128)S(1)}, f32[512,2048]{1,0:T(8,128)}, u32[]{:S(2)}, u32[]{:S(2)}) collective-permute-start(f32[512,2048]{1,0:T(8,128)S(1)} %collective-permute-done), channel_id=1, source_target_pairs={{0,8},{8,16},{16,24},{24,0},{1,9},{9,17},{17,25},{25,1},{2,10},{10... | collective-permute-start | bytes 12582920 | tf_op jit(solution)/shard_map/ppermute | solution.py:85
  679.4 183.3 %collective-permute-start.2 = (f32[512,2048]{1,0:T(8,128)}, f32[512,2048]{1,0:T(8,128)}, u32[]{:S(2)}, u32[]{:S(2)}) collective-permute-start(f32[512,2048]{1,0:T(8,128)} %collective-permute-done.1), channel_id=1, source_target_pairs={{0,8},{8,16},{16,24},{24,0},{1,9},{9,17},{17,25},{25,1},{2,10},{10... | collective-permute-start | bytes 12582920 | tf_op jit(solution)/shard_map/ppermute | solution.py:85
  697.1 557.7 %reduce-scatter.2.cloned.1.call-start = ((), (), s32[]{:S(2)}) async-start(), calls=%async_computation.4 | async-start | bytes 41943040 | tf_op jit(solution)/shard_map/reduce_scatter | solution.py:14
  697.2 175.2 %copy-start.4 = (f32[512,2048]{1,0:T(8,128)S(1)}, f32[512,2048]{1,0:T(8,128)}, u32[]{:S(2)}) copy-start(f32[512,2048]{1,0:T(8,128)} %copy-done.3) | copy-start | bytes 12582916
  867.5 7.1 copy-start.2
  1024.4 400.7 %all-gather.18.cloned.1.call-start = ((), (), s32[]{:S(2)}) async-start(), calls=%async_computation.6 | async-start | bytes 35651584 | tf_op jit(solution)/shard_map/all_gather | solution.py:99
Sparse Core Ops, SparseCore 0:
  9.5 106.6 all-gather.19
  117.8 286.7 all-gather.21
  406.2 54.8 all-gather.9
  463.1 103.9 all-gather.13
  568.6 308.9 all-gather.11
  879.5 54.4 all-gather.15
  1024.5 230.2 reduce-scatter.1
  1257.0 168.0 all-gather.17
